TPU v7x, 32 devices: a 4x4x1 block of a 4x4x8 slice. The times are simulated.
32 devices in a mesh: rep: 2 (over z, core), dp: 16 (over x, y).
Axes of the slice: x: 4, y: 4, z: 1, core: 2. Of those that a mesh axis runs over, the one named last changes fastest.
The devices are a block of a 4x4x8 slice.
Arguments:
- g_w_gate: bfloat16 [32, 2, 1024, 3200], P(('rep', 'dp')), parts along dimension 0
- g_w_up: bfloat16 [32, 2, 1024, 3200], P(('rep', 'dp')), parts along dimension 0
- g_w_down: bfloat16 [32, 2, 3200, 1024], P(('rep', 'dp')), parts along dimension 0
- w_gate: bfloat16 [2, 1024, 3200], replicated
- w_up: bfloat16 [2, 1024, 3200], replicated
- w_down: bfloat16 [2, 3200, 1024], replicated
- m_w_gate: float32 [2, 1024, 3200], P(None, 'dp')
- m_w_up: float32 [2, 1024, 3200], P(None, 'dp')
- m_w_down: float32 [2, 3200, 1024], P(None, 'dp')
- v_w_gate: float32 [2, 1024, 3200], P(None, 'dp')
- v_w_up: float32 [2, 1024, 3200], P(None, 'dp')
- v_w_down: float32 [2, 3200, 1024], P(None, 'dp')
Outputs:
- output 1: bfloat16 [4, 1024, 3200], P('rep'), parts along dimension 0
- output 2: bfloat16 [4, 1024, 3200], P('rep'), parts along dimension 0
- output 3: bfloat16 [4, 3200, 1024], P('rep'), parts along dimension 0
- output 4: float32 [4, 1024, 3200], P('rep', 'dp'), parts along dimension 0
- output 5: float32 [4, 1024, 3200], P('rep', 'dp'), parts along dimension 0
- output 6: float32 [4, 3200, 1024], P('rep', 'dp'), parts along dimension 0
- output 7: float32 [4, 1024, 3200], P('rep', 'dp'), parts along dimension 0
- output 8: float32 [4, 1024, 3200], P('rep', 'dp'), parts along dimension 0
- output 9: float32 [4, 3200, 1024], P('rep', 'dp'), parts along dimension 0
There are 2 independent parts. A program takes and returns all parts, laid end to end along the dimension named above; an argument that names none is the same for every part.
All inputs are finite; a program needn't handle non-finite values.
Results may differ from a plain program's by a relative error of at most 0.022.
Values are sent between devices in bfloat16 or wider.
A program may use at most 768 MiB of HBM per device.

v0:
```python
import jax
import jax.numpy as jnp
from jax import lax
from jax.sharding import PartitionSpec as P


def adamw(w, m, v, g):
    m = 0.9 * m + 0.1 * g
    v = 0.95 * v + 0.05 * g * g
    step = m * lax.rsqrt(v + 1e-8) + 0.1 * w
    return (w - 0.02 * step).astype(jnp.bfloat16), m, v


def solution(mesh):
    def step(*arrays):
        terms, weights, m, v = (arrays[i : i + 3] for i in (0, 3, 6, 9))
        gradients = [lax.psum_scatter(t[0], "dp", scatter_dimension=1, tiled=True).astype(jnp.float32) for t in terms]
        me = lax.axis_index("dp")
        own = [lax.dynamic_slice_in_dim(w, me * one.shape[1], one.shape[1], 1).astype(jnp.float32) for w, one in zip(weights, m, strict=True)]
        new = [adamw(w, m, v, g) for w, m, v, g in zip(own, m, v, gradients, strict=True)]
        whole = [lax.all_gather(one[0], "dp", axis=1, tiled=True) for one in new]
        return (*whole, *(one[1] for one in new), *(one[2] for one in new))

    all_of, cut = P(None, None, None), P(None, "dp", None)
    return jax.shard_map(
        step,
        mesh=mesh,
        in_specs=(P(("rep", "dp"), None, None, None),) * 3 + (all_of,) * 3 + (cut,) * 6,
        out_specs=(P("rep", None, None),) * 3 + (P("rep", "dp", None),) * 6,
        check_vma=False,
    )
```

profile of v0, /device:TPU:97, one launch (start us, length us, event | category | flops | bytes accessed | tf_op | source)
XLA Modules:
  0.0 674.3 jit_solution(12461627571111590454)
XLA Ops:
  7.2 0.1 all-reduce.3.cloned.1.call-start
  7.3 0.7 all-reduce.3.cloned.1.call-update
  8.0 0.1 reduce-scatter.6.cloned.1.call-start
  8.1 0.7 reduce-scatter.6.cloned.1.call-update
  8.8 0.1 reduce-scatter.4.cloned.1.call-start
  8.9 0.0 copy-start.5
  8.9 0.0 copy-start.1
  8.9 0.0 copy-start.2
  8.9 0.7 reduce-scatter.4.cloned.1.call-update
  9.6 0.1 all-gather.8.cloned.1.call-start
  9.7 0.0 copy-done.5
  9.7 0.6 dynamic-slice
  10.9 177.1 %all-reduce.3.cloned.1.call-done = bf16[2,3200,1024]{2,1,0:T(8,128)(2,1)} async-done(((bf16[2,3200,1024]{2,1,0:T(8,128)(2,1)}), bf16[2,3200,1024]{2,1,0:T(8,128)(2,1)}) %all-reduce.3.cloned.1.call-update) | async-done | bytes 13107216
  188.0 0.0 copy-done.1
  188.0 0.0 copy-done.2
  188.0 3.9 fusion.10
  191.9 0.1 all-gather.8.cloned.1.call-update
  192.0 0.1 all-gather.6.cloned.1.call-start
  192.0 88.6 %reduce-scatter.6.cloned.1.call-done = bf16[2,64,3200]{2,1,0:T(8,128)(2,1)} async-done(((bf16[2,1024,3200]{2,1,0:T(8,128)(2,1)}), bf16[2,64,3200]{2,1,0:T(8,128)(2,1)}) %reduce-scatter.6.cloned.1.call-update) | async-done | bytes 819216 | tf_op jit(solution)/shard_map/reduce_scatter | solution.py:17
  280.6 0.0 copy-start.3
  280.6 0.0 copy-start.4
  280.6 4.9 fusion.6
  285.6 0.1 all-gather.6.cloned.1.call-update
  285.6 0.1 all-gather.4.cloned.1.call-start
  285.7 87.5 %reduce-scatter.4.cloned.1.call-done = bf16[2,64,3200]{2,1,0:T(8,128)(2,1)} async-done(((bf16[2,1024,3200]{2,1,0:T(8,128)(2,1)}), bf16[2,64,3200]{2,1,0:T(8,128)(2,1)}) %reduce-scatter.4.cloned.1.call-update) | async-done | bytes 819216 | tf_op jit(solution)/shard_map/reduce_scatter | solution.py:17
  373.2 0.0 copy-done.3
  373.2 0.0 copy-done.4
  373.2 3.8 fusion.2
  377.0 0.1 all-gather.4.cloned.1.call-update
  377.0 85.4 %all-gather.8.cloned.1.call-done = bf16[2,3200,1024]{2,1,0:T(8,128)(2,1)} async-done(((bf16[2,200,1024]{2,1,0:T(8,128)(2,1)}), bf16[2,3200,1024]{2,1,0:T(8,128)(2,1)}) %all-gather.8.cloned.1.call-update) | async-done | bytes 13107216 | tf_op jit(solution)/shard_map/all_gather | solution.py:21
  462.5 89.1 %all-gather.6.cloned.1.call-done = bf16[2,1024,3200]{2,1,0:T(8,128)(2,1)} async-done(((bf16[2,64,3200]{2,1,0:T(8,128)(2,1)}), bf16[2,1024,3200]{2,1,0:T(8,128)(2,1)}) %all-gather.6.cloned.1.call-update) | async-done | bytes 13107216 | tf_op jit(solution)/shard_map/all_gather | solution.py:21
  551.6 89.1 %all-gather.4.cloned.1.call-done = bf16[2,1024,3200]{2,1,0:T(8,128)(2,1)} async-done(((bf16[2,64,3200]{2,1,0:T(8,128)(2,1)}), bf16[2,1024,3200]{2,1,0:T(8,128)(2,1)}) %all-gather.4.cloned.1.call-update) | async-done | bytes 13107216 | tf_op jit(solution)/shard_map/all_gather | solution.py:21
  640.7 0.0 copy-start
  640.7 0.0 slice-start
  640.7 0.0 slice-start.1
  640.7 12.7 %copy.28 = bf16[2,1024,3200]{2,1,0:T(8,128)(2,1)} copy(bf16[2,1024,3200]{2,1,0:T(8,128)(2,1)} %all-gather.4.cloned.1.call-done) | data formatting | bytes 26214400
  653.4 0.0 copy-done
  653.4 0.0 slice-start.2
  653.4 0.0 slice-start.3
  653.4 6.6 copy.29
  660.0 0.0 slice-done
  660.0 1.2 slice-done.1
  661.2 1.3 slice-done.2
  662.5 0.0 slice-done.3
  662.5 4.9 copy.30
  (1 shorter events, 0.0 us)
Async XLA Ops:
  7.2 180.8 %all-reduce.3.cloned.1.call-start = ((), (), s32[]{:S(2)}) async-start(), calls=%async_computation.7 | async-start | bytes 26214400
  8.0 272.6 %reduce-scatter.6.cloned.1.call-start = ((), (), s32[]{:S(2)}) async-start(), calls=%async_computation.4 | async-start | bytes 13926400 | tf_op jit(solution)/shard_map/reduce_scatter | solution.py:17
  8.8 364.4 %reduce-scatter.4.cloned.1.call-start = ((), (), s32[]{:S(2)}) async-start(), calls=%async_computation.2 | async-start | bytes 13926400 | tf_op jit(solution)/shard_map/reduce_scatter | solution.py:17
  8.9 0.8 copy-start.5
  8.9 179.1 %copy-start.1 = (f32[2,200,1024]{2,1,0:T(8,128)S(1)}, f32[2,200,1024]{2,1,0:T(8,128)}, u32[]{:S(2)}) copy-start(f32[2,200,1024]{2,1,0:T(8,128)} %param.23) | copy-start | bytes 4915204
  8.9 179.1 %copy-start.2 = (f32[2,200,1024]{2,1,0:T(8,128)S(1)}, f32[2,200,1024]{2,1,0:T(8,128)}, u32[]{:S(2)}) copy-start(f32[2,200,1024]{2,1,0:T(8,128)} %param.20) | copy-start | bytes 4915204
  9.6 452.9 %all-gather.8.cloned.1.call-start = ((), (), s32[]{:S(2)}) async-start(), calls=%async_computation.6 | async-start | bytes 13926400 | tf_op jit(solution)/shard_map/all_gather | solution.py:21
  192.0 359.6 %all-gather.6.cloned.1.call-start = ((), (), s32[]{:S(2)}) async-start(), calls=%async_computation.5 | async-start | bytes 13926400 | tf_op jit(solution)/shard_map/all_gather | solution.py:21
  280.6 92.6 %copy-start.3 = (f32[2,64,3200]{2,1,0:T(8,128)S(1)}, f32[2,64,3200]{2,1,0:T(8,128)}, u32[]{:S(2)}) copy-start(f32[2,64,3200]{2,1,0:T(8,128)} %param.21) | copy-start | bytes 4915204
  280.6 92.6 %copy-start.4 = (f32[2,64,3200]{2,1,0:T(8,128)S(1)}, f32[2,64,3200]{2,1,0:T(8,128)}, u32[]{:S(2)}) copy-start(f32[2,64,3200]{2,1,0:T(8,128)} %param.18) | copy-start | bytes 4915204
  285.6 355.1 %all-gather.4.cloned.1.call-start = ((), (), s32[]{:S(2)}) async-start(), calls=%async_computation.3 | async-start | bytes 13926400 | tf_op jit(solution)/shard_map/all_gather | solution.py:21
  640.7 12.7 %copy-start = (bf16[2,1024,3200]{2,1,0:T(8,128)(2,1)S(1)}, bf16[2,1024,3200]{2,1,0:T(8,128)(2,1)}, u32[]{:S(2)}) copy-start(bf16[2,1024,3200]{2,1,0:T(8,128)(2,1)} %all-gather.6.cloned.1.call-done) | copy-start | bytes 39321604
  640.7 19.4 %slice-start = ((s8[13107200]{0:T(1024)(128)(4,1)}), s8[4194304]{0:T(1024)(128)(4,1)S(1)}, s32[]{:S(2)}) async-start(s8[13107200]{0:T(1024)(128)(4,1)} %bitcast.9), calls=%async_computation.8 | async-start | bytes 8388608
  640.7 20.5 %slice-start.1 = ((s8[13107200]{0:T(1024)(128)(4,1)}), s8[4194304]{0:T(1024)(128)(4,1)S(1)}, s32[]{:S(2)}) async-start(s8[13107200]{0:T(1024)(128)(4,1)} %bitcast.9), calls=%async_computation.9 | async-start | bytes 8388608
  653.4 9.1 %slice-start.2 = ((s8[13107200]{0:T(1024)(128)(4,1)}), s8[4194304]{0:T(1024)(128)(4,1)S(1)}, s32[]{:S(2)}) async-start(s8[13107200]{0:T(1024)(128)(4,1)} %bitcast.9), calls=%async_computation.10 | async-start | bytes 8388608
  653.4 9.1 %slice-start.3 = ((s8[13107200]{0:T(1024)(128)(4,1)}), s8[524288]{0:T(1024)(128)(4,1)S(1)}, s32[]{:S(2)}) async-start(s8[13107200]{0:T(1024)(128)(4,1)} %bitcast.9), calls=%async_computation.11 | async-start | bytes 1048576
Sparse Core Ops, SparseCore 0:
  11.7 176.2 all-reduce.2
  191.3 89.2 reduce-scatter.5
  283.9 89.2 reduce-scatter.3
  375.6 86.8 all-gather.7
  464.8 86.6 all-gather.5
  554.0 86.6 all-gather.3
where the time goes:
time: 674 us
  waiting for transfers between devices  619 us (92%)
  local copies, waits for them, and re-layouts  27.4 us (4%)
  between operations  14.8 us (2%)
  other arithmetic  12.6 us (2%)
    all_gather x3, waiting for transfers between devices, step(): whole = [lax.all_gather(one[0], 'dp', axis=1, tiled=True) for one in new]  264 us
    unnamed x7, waiting for transfers between devices  179 us
    reduce_scatter x2, waiting for transfers between devices, step(): lax.psum_scatter(t[0], 'dp', scatter_dimension=1, tiled=True)  176 us
    unnamed x24, local copies, waits for them, and re-layouts  27.4 us
  transfers between devices with their start and end apart: 6, of which 6 were waited for; matrix products, arithmetic and copies ran while one was open for 2% of the time, Pallas kernels for 0%

commit v1 on v0

v1 whole, which is shorter than its diff:
```python
import functools
import math

import jax
import jax.numpy as jnp
from jax import lax
from jax.experimental import pallas as pl
from jax.experimental.pallas import tpu as pltpu
from jax.sharding import PartitionSpec as P

MESH = pl.DeviceIdType.MESH
S1, S2A, S2B, T1, T2A, T2B, A1, A1F, A2, A2F = range(10)
KINDS = 10
STAGES = 9


def halves(shape):
    rows, columns = shape
    if rows % 32 == 0:
        return (rows // 4, columns), lambda i, n=1: (pl.ds(i * (rows // 4), n * (rows // 4)), slice(None))
    return (rows, columns // 4), lambda i, n=1: (slice(None), pl.ds(i * (columns // 4), n * (columns // 4)))


def pieces(shape):
    rows, columns = shape
    if rows <= 64:
        n = next(k for k in (5, 3, 2, 1) if columns % (k * 128) == 0)
        return n, lambda i: (slice(None), pl.ds(pl.multiple_of(i * (columns // n), 128), columns // n))
    n = next(k for k in (5, 4, 2, 1) if rows % (k * 8) == 0)
    return n, lambda i: (pl.ds(pl.multiple_of(i * (rows // n), 8), rows // n), slice(None))


def kernel(side, layers, shapes, *refs):
    n = len(shapes)
    gs, ws, ms, vs, outs, gouts = (refs[i * n : (i + 1) * n] for i in range(6))
    scratch = refs[6 * n : -4]
    send, recv, local, stored = refs[-4:]
    kinds = list(dict.fromkeys(shapes))
    per = len(scratch) // len(kinds)
    held = {shape: scratch[i * per : (i + 1) * per] for i, shape in enumerate(kinds)}
    jobs, seen = [], {shape: 0 for shape in kinds}
    for which, shape in enumerate(shapes):
        for layer in range(layers):
            jobs.append((which, layer, shape, seen[shape]))
            seen[shape] += 1

    me = lax.axis_index("dp")
    xy = (lax.div(me, side), lax.rem(me, side))

    def at(i, by):
        return lax.rem(i + (by + side), side)

    def place(c):
        return xy[c], xy[1 - c]

    def pair(c, p, s):
        return (p, s) if c == 0 else (s, p)

    def device(c, p, s):
        a, b = pair(c, p, s)
        return {"dp": a * side + b}

    signs = (1, -1)
    barrier = pltpu.get_barrier_semaphore()
    for c in range(2):
        p, s = place(c)
        for by in signs:
            pl.semaphore_signal(barrier, inc=1, device_id=device(c, at(p, by), s), device_id_type=MESH)
    pl.semaphore_wait(barrier, 4)

    def copy(q, c, d, kind):
        which, layer, shape, slot = jobs[q]
        r1, r2, q1, q2, oc, ob, mb, vb, wb, wn = held[shape]
        quarter, index = halves(shape)
        g, out = gs[which], outs[which]
        p, s = place(c)
        by = signs[d]

        def chunk(i, h):
            return g.at[(layer, i, slice(None), *index(2 * c + h))] if c == 0 else g.at[(layer, slice(None), i, *index(2 * c + h))]

        def block(i, j, h=0, width=2):
            return out.at[(layer, *pair(c, i, j), *index(2 * c + h, width))]

        def row(i, h=0, width=2):
            return block(i, slice(None), h, width)

        along = device(c, at(p, by), s)
        across = device(c, p, at(s, by))
        if kind == S1:
            src, dst, to = chunk(at(p, 2), d), r1.at[slot, c, d], along
        elif kind == S2A:
            src, dst, to = chunk(at(p, by), 1 - d), r2.at[slot, c, d, 1 - d], along
        elif kind == S2B:
            src, dst, to = r1.at[slot, c, d], r2.at[slot, c, d, d], along
        elif kind == T1:
            src, dst, to = oc.at[slot, c, d, at(s, 2)], q1.at[slot, c, d], across
        elif kind == T2A:
            src, dst, to = oc.at[slot, c, 1 - d, at(s, by)], q2.at[slot, c, d, 1 - d], across
        elif kind == T2B:
            src, dst, to = q1.at[slot, c, d], q2.at[slot, c, d, d], across
        elif kind == A1:
            src, dst, to = wn.at[slot, c], block(p, s), across
        elif kind == A1F:
            src, dst, to = block(p, at(s, -by), d, 1), block(p, at(s, -by), d, 1), across
        elif kind == A2:
            src, dst, to = row(p), row(p), along
        else:
            src, dst, to = row(at(p, -by), d, 1), row(at(p, -by), d, 1), along
        return pltpu.make_async_remote_copy(
            src_ref=src,
            dst_ref=dst,
            send_sem=send.at[q, c, d, kind],
            recv_sem=recv.at[q, c, d, kind],
            device_id=to,
            device_id_type=MESH,
        )

    each = [(c, d) for c in range(2) for d in range(2)]

    def start(q, kind):
        for c, d in each:
            copy(q, c, d, kind).start()

    def arrived(q, kind):
        for c, d in each:
            copy(q, c, d, kind).wait_recv()

    def own(q, c, d, kept):
        which, layer, shape, slot = jobs[q]
        oc, ob = held[shape][4:6]
        _, index = halves(shape)
        p, _ = place(c)
        g = gs[which]

        def chunk(i, h):
            return g.at[(layer, i, slice(None), *index(2 * c + h))] if c == 0 else g.at[(layer, slice(None), i, *index(2 * c + h))]

        if kept:
            return pltpu.make_async_copy(chunk(p, d), oc.at[slot, c, d], local.at[q, 4 + 2 * c + d])
        return pltpu.make_async_copy(chunk(at(p, signs[d]), d), ob.at[slot % 2, c, d], local.at[q, 2 * c + d])

    def state(q):
        which, layer, shape, slot = jobs[q]
        mb, vb, wb = held[shape][6:9]
        sources = (ms[which].at[layer], vs[which].at[layer], ws[which].at[layer, xy[0], xy[1]])
        return [
            pltpu.make_async_copy(src, buffer.at[slot % 2], local.at[q, 8 + i])
            for i, (src, buffer) in enumerate(zip(sources, (mb, vb, wb), strict=True))
        ]

    def weight(q, c):
        which, layer, shape, slot = jobs[q]
        mine = outs[which].at[(layer, xy[0], xy[1], *halves(shape)[1](2 * c, 2))]
        return pltpu.make_async_copy(held[shape][9].at[slot, c], mine, stored.at[q, c, 2])

    def gradient(q, c, h):
        which, layer, shape, slot = jobs[q]
        mine = gouts[which].at[(layer, *halves(shape)[1](2 * c + h))]
        return pltpu.make_async_copy(held[shape][3].at[slot, c, 0, h], mine, stored.at[q, c, h])

    def walk(shape, body):
        steps, piece = pieces(halves(shape)[0])

        @pl.loop(0, steps)
        def _(i):
            body(piece(i))

    def add(shape, *todo):
        def body(where):
            for (ref, lead), terms in todo:
                parts = [t[(*at_, *where)].astype(jnp.float32) for t, at_ in terms]
                ref[(*lead, *where)] = functools.reduce(lambda a, b: a + b, parts).astype(ref.dtype)

        walk(shape, body)

    def stage(k, q):
        which, layer, shape, slot = jobs[q]
        r1, r2, q1, q2, oc, ob, mb, vb, wb, wn = held[shape]
        _, index = halves(shape)
        if k == 0:
            start(q, S1)
            start(q, S2A)
            for c, d in each:
                own(q, c, d, False).start()
                own(q, c, d, True).start()
        elif k == 1:
            for c, d in each:
                copy(q, c, d, S1).wait_recv()
                own(q, c, d, False).wait()

                @pl.loop(0, side)
                def _(j, c=c, d=d):
                    there = (slot, c, d, j)
                    add(shape, ((r1, there), ((r1, there), (ob, (slot % 2, c, d, j)))))

                copy(q, c, d, S2B).start()
        elif k == 2:
            arrived(q, S2A)
            arrived(q, S2B)
            for c, d in each:
                own(q, c, d, True).wait()
            for c in range(2):
                s = place(c)[1]
                for h, j in ((0, at(s, 2)), (1, at(s, 2)), (1, at(s, 1)), (0, at(s, -1))):
                    here = (slot, c, h, j)
                    add(shape, ((oc, here), ((oc, here), (r2, (slot, c, 0, h, j)), (r2, (slot, c, 1, h, j)))))
            start(q, T1)
            start(q, T2A)
        elif k == 3:
            for one in state(q):
                one.start()
            for c, d in each:
                s = place(c)[1]
                copy(q, c, d, T1).wait_recv()
                j = at(s, signs[d])
                here = (slot, c, d)
                add(shape, ((q1, here), ((oc, (*here, j)), (r2, (slot, c, 0, d, j)), (r2, (slot, c, 1, d, j)), (q1, here))))
                copy(q, c, d, T2B).start()
        elif k == 4:
            arrived(q, T2A)
            arrived(q, T2B)
            for one in state(q):
                one.wait()
            for c in range(2):
                s = place(c)[1]
                for h in range(2):
                    terms = [(oc, (slot, c, h, s))] + [(r2, (slot, c, d, h, s)) for d in range(2)] + [(q2, (slot, c, d, h)) for d in range(2)]
                    quarter = index(2 * c + h)
                    offsets = [x.start if isinstance(x, pl.Slice) else 0 for x in quarter]
                    half = [x.start if isinstance(x, pl.Slice) else 0 for x in index(h)]

                    def body(where, c=c, h=h, terms=terms, offsets=offsets, half=half):
                        def shifted(by):
                            full = []
                            for w, size, o in zip(where, halves(shape)[0], by, strict=True):
                                full.append(pl.ds(o, size) if isinstance(w, slice) else pl.ds(o + w.start, w.size))
                            return tuple(full)

                        g = functools.reduce(lambda a, b: a + b, [t[(*lead, *where)].astype(jnp.float32) for t, lead in terms])
                        g16 = g.astype(jnp.bfloat16)
                        g = g16.astype(jnp.float32)
                        q2[(slot, c, 0, h, *where)] = g16
                        there = (slot % 2, *shifted(offsets))
                        w = wb[there].astype(jnp.float32)
                        m = 0.9 * mb[there] + 0.1 * g
                        v = 0.95 * vb[there] + 0.05 * g * g
                        new = w - 0.02 * (m * lax.rsqrt(v + 1e-8) + 0.1 * w)
                        wn[(slot, c, *shifted(half))] = new.astype(jnp.bfloat16)

                    walk(shape, body)
                for d in range(2):
                    copy(q, c, d, A1).start()
                weight(q, c).start()
                for h in range(2):
                    gradient(q, c, h).start()
        elif k == 5:
            arrived(q, A1)
            start(q, A1F)
        elif k == 6:
            for c in range(2):
                weight(q, c).wait()
            arrived(q, A1F)
            start(q, A2)
        elif k == 7:
            arrived(q, A2)
            start(q, A2F)
        else:
            arrived(q, A2F)

    for t in range(len(jobs) + STAGES - 1):
        for k in range(STAGES):
            if 0 <= t - k < len(jobs):
                stage(k, t - k)

    for q in range(len(jobs)):
        for c in range(2):
            for h in range(2):
                gradient(q, c, h).wait()
        for kind in range(KINDS):
            for c, d in each:
                copy(q, c, d, kind).wait_send()


def step_kernel(side, layers, shapes, terms, weights, m, v):
    scratch = []
    for shape in dict.fromkeys(shapes):
        count = layers * shapes.count(shape)
        quarter, _ = halves(shape)
        both = (quarter[0] * 2, quarter[1]) if quarter[1] == shape[1] else (quarter[0], quarter[1] * 2)
        scratch += [
            pltpu.VMEM((count, 2, 2, side, *quarter), jnp.bfloat16),
            pltpu.VMEM((count, 2, 2, 2, side, *quarter), jnp.bfloat16),
            pltpu.VMEM((count, 2, 2, *quarter), jnp.bfloat16),
            pltpu.VMEM((count, 2, 2, 2, *quarter), jnp.bfloat16),
            pltpu.VMEM((count, 2, 2, side, *quarter), jnp.bfloat16),
            pltpu.VMEM((2, 2, 2, side, *quarter), jnp.bfloat16),
            pltpu.VMEM((2, *shape), jnp.float32),
            pltpu.VMEM((2, *shape), jnp.float32),
            pltpu.VMEM((2, *shape), jnp.bfloat16),
            pltpu.VMEM((count, 2, *both), jnp.bfloat16),
        ]
    jobs = layers * len(shapes)
    anywhere = pl.BlockSpec(memory_space=pl.ANY)
    return pl.pallas_call(
        functools.partial(kernel, side, layers, shapes),
        out_shape=[jax.ShapeDtypeStruct(w.shape, jnp.bfloat16) for w in weights]
        + [jax.ShapeDtypeStruct(one.shape, jnp.bfloat16) for one in m],
        in_specs=[anywhere] * (4 * len(shapes)),
        out_specs=[anywhere] * (2 * len(shapes)),
        scratch_shapes=scratch
        + [
            pltpu.SemaphoreType.DMA((jobs, 2, 2, KINDS)),
            pltpu.SemaphoreType.DMA((jobs, 2, 2, KINDS)),
            pltpu.SemaphoreType.DMA((jobs, 11)),
            pltpu.SemaphoreType.DMA((jobs, 2, 3)),
        ],
        compiler_params=pltpu.CompilerParams(collective_id=0, has_side_effects=True, vmem_limit_bytes=67_043_328),
        name="step",
    )(*terms, *weights, *m, *v)


def solution(mesh):
    side = math.isqrt(mesh.shape["dp"])

    def step(*arrays):
        terms, weights, m, v = (arrays[i : i + 3] for i in (0, 3, 6, 9))
        shapes = tuple(one.shape[1:] for one in m)
        layers = m[0].shape[0]
        split = [(layers, side, side, *shape) for shape in shapes]
        *new, g0, g1, g2 = step_kernel(
            side,
            layers,
            shapes,
            [t[0].reshape(s) for t, s in zip(terms, split, strict=True)],
            [w.reshape(s) for w, s in zip(weights, split, strict=True)],
            m,
            v,
        )
        whole = [one.reshape(w.shape) for one, w in zip(new, weights, strict=True)]
        g = [one.astype(jnp.float32) for one in (g0, g1, g2)]
        return (
            *whole,
            *(0.9 * a + 0.1 * b for a, b in zip(m, g, strict=True)),
            *(0.95 * a + 0.05 * b * b for a, b in zip(v, g, strict=True)),
        )

    all_of, cut = P(None, None, None), P(None, "dp", None)
    return jax.shard_map(
        step,
        mesh=mesh,
        in_specs=(P(("rep", "dp"), None, None, None),) * 3 + (all_of,) * 3 + (cut,) * 6,
        out_specs=(P("rep", None, None),) * 3 + (P("rep", "dp", None),) * 6,
        check_vma=False,
    )
```

time: 674 us -> 445 us (0.66)
  waiting for transfers between devices: 619 us -> 0 us
  Pallas kernels: 0 us -> 409 us
  between operations: 14.8 us -> 0.7 us
    pallas_call x0 -> x1, Pallas kernels: none -> 409 us  [step_kernel(): pl.pallas_call(functools.partial(kernel, side, layers, shapes), out_shape...]
    all_gather x3 -> x0, waiting for transfers between devices: 264 us -> none  [step(): whole = [lax.all_gather(one[0], 'dp', axis=1, tiled=True) for one in new]]
    unnamed x7 -> x0, waiting for transfers between devices: 179 us -> none
    reduce_scatter x2 -> x0, waiting for transfers between devices: 176 us -> none  [step(): lax.psum_scatter(t[0], 'dp', scatter_dimension=1, tiled=True)]
    convert_element_type x3 -> x0, other arithmetic: 12.6 us -> none  [adamw(): return ((w - 0.02 * step).astype(jnp.bfloat16), m, v)]
    add x0 -> x2, other arithmetic: none -> 12 us  [step(): 0.95 * a + 0.05 * b * b]
    unnamed x24 -> x17, local copies, waits for them, and re-layouts: 27.4 us -> 23 us
  transfers between devices with their start and end apart: 6 -> 0, of which waited for: 6 -> 0; matrix products, arithmetic and copies ran while one was open for 2% -> 0% of each run, Pallas kernels for 0% -> 0%
where the time goes in v1:
time: 445 us
  Pallas kernels  409 us (92%)
  local copies, waits for them, and re-layouts  23 us (5%)
  other arithmetic  12 us (3%)
    pallas_call x1, Pallas kernels, step_kernel(): pl.pallas_call(functools.partial(kernel, side, layers, shapes), out_shape...  409 us
    unnamed x17, local copies, waits for them, and re-layouts  23 us
    add x2, other arithmetic, step(): 0.95 * a + 0.05 * b * b  12 us

profile of v1, /device:TPU:97, one launch (start us, length us, event | category | flops | bytes accessed | tf_op | source)
XLA Modules:
  0.0 444.8 jit_solution(15691151243710057375)
XLA Ops:
  0.6 409.1 %step.1 = (bf16[2,4,4,64,3200]{4,3,2,1,0:T(8,128)(2,1)}, bf16[2,4,4,64,3200]{4,3,2,1,0:T(8,128)(2,1)}, bf16[2,4,4,200,1024]{4,3,2,1,0:T(8,128)(2,1)}, bf16[2,64,...) custom-call(bf16[2,4,4,64,3200]{4,3,2,1,0:T(8,128)(2,1)} %bitcast.14, ...), custom_call_target="tpu_custom_call" | custom-call | tf_op jit(solution)/shard_map/step/pallas_call | solution.py:305
  409.7 0.0 copy-start.2
  409.7 0.0 copy-start.1
  409.8 7.1 %fusion.3 = (f32[2,64,3200]{2,1,0:T(8,128)}, f32[2,64,3200]{2,1,0:T(8,128)}, f32[2,64,3200]{2,1,0:T(8,128)}, f32[2,64,3200]{2,1,0:T(8,128)}) fusion(bf16[2,64,3200]{2,1,0:T(8,128)(2,1)} %get-tuple-element.18, f32[2,64,3200]{2,1,0:T(8,128)} %refs_9_.1, f32[2,64,3200]{2,1,0:T(8,128)} %refs_6_.1, bf16[2,64,3200]{2,1,0:T(8,128)(2,1)} %get-tuple-element.19, ...), kind=kLoop, calls=%fused_computation.9 | loop fusion | flops 6553600 | bytes 14745600 | tf_op jit(solution)/shard_map/add | solution.py:345
  416.8 0.0 copy-done.2
  416.8 4.9 %fusion.5 = (f32[2,200,1024]{2,1,0:T(8,128)}, f32[2,200,1024]{2,1,0:T(8,128)}) fusion(bf16[2,200,1024]{2,1,0:T(8,128)(2,1)} %get-tuple-element.20, f32[2,200,1024]{2,1,0:T(8,128)} %refs_11_.1, f32[2,200,1024]{2,1,0:T(8,128)S(1)} %copy-done.2), kind=kLoop, calls=%fused_computation.11 | loop fusion | flops 3276800 | bytes 7372800 | tf_op jit(solution)/shard_map/add | solution.py:345
  421.8 0.0 copy-done.1
  421.8 0.0 copy-start
  421.8 0.0 slice-start
  421.8 0.0 slice-start.1
  421.8 0.0 slice-start.2
  421.8 6.6 %copy.24 = bf16[2,1024,3200]{2,1,0:T(8,128)(2,1)} copy(bf16[2,1024,3200]{2,1,0:T(8,128)(2,1)S(1)} %bitcast.13) | data formatting | bytes 26214400
  428.4 2.8 copy-done
  431.2 0.0 slice-start.3
  431.2 6.6 %copy.25 = bf16[2,1024,3200]{2,1,0:T(8,128)(2,1)} copy(bf16[2,1024,3200]{2,1,0:T(8,128)(2,1)S(1)} %bitcast.12) | data formatting | bytes 26214400
  437.9 0.0 slice-done
  437.9 0.0 slice-done.1
  437.9 1.7 slice-done.2
  439.5 0.3 slice-done.3
  439.8 4.9 %copy.26 = bf16[2,3200,1024]{2,1,0:T(8,128)(2,1)} copy(bf16[2,3200,1024]{2,1,0:T(8,128)(2,1)S(1)} %bitcast.11) | data formatting | bytes 26214400
  (1 shorter events, 0.0 us)
Async XLA Ops:
  409.7 7.1 %copy-start.2 = (f32[2,200,1024]{2,1,0:T(8,128)S(1)}, f32[2,200,1024]{2,1,0:T(8,128)}, u32[]{:S(2)}) copy-start(f32[2,200,1024]{2,1,0:T(8,128)} %refs_8_.1) | copy-start | bytes 4915204
  409.7 12.0 %copy-start.1 = (bf16[2,4,4,64,3200]{4,3,2,1,0:T(8,128)(2,1)S(1)}, bf16[2,4,4,64,3200]{4,3,2,1,0:T(8,128)(2,1)}, u32[]{:S(2)}) copy-start(bf16[2,4,4,64,3200]{4,3,2,1,0:T(8,128)(2,1)} %get-tuple-element.15) | copy-start | bytes 39321604
  421.8 9.5 %copy-start = (bf16[2,4,4,64,3200]{4,3,2,1,0:T(8,128)(2,1)S(1)}, bf16[2,4,4,64,3200]{4,3,2,1,0:T(8,128)(2,1)}, u32[]{:S(2)}) copy-start(bf16[2,4,4,64,3200]{4,3,2,1,0:T(8,128)(2,1)} %get-tuple-element.16) | copy-start | bytes 39321604
  421.8 16.1 %slice-start = ((s8[13107200]{0:T(1024)(128)(4,1)}), s8[4194304]{0:T(1024)(128)(4,1)S(1)}, s32[]{:S(2)}) async-start(s8[13107200]{0:T(1024)(128)(4,1)} %bitcast.9), calls=%async_computation | async-start | bytes 8388608
  421.8 16.1 %slice-start.1 = ((s8[13107200]{0:T(1024)(128)(4,1)}), s8[4194304]{0:T(1024)(128)(4,1)S(1)}, s32[]{:S(2)}) async-start(s8[13107200]{0:T(1024)(128)(4,1)} %bitcast.9), calls=%async_computation.1 | async-start | bytes 8388608
  421.8 17.8 %slice-start.2 = ((s8[13107200]{0:T(1024)(128)(4,1)}), s8[4194304]{0:T(1024)(128)(4,1)S(1)}, s32[]{:S(2)}) async-start(s8[13107200]{0:T(1024)(128)(4,1)} %bitcast.9), calls=%async_computation.2 | async-start | bytes 8388608
  431.2 8.6 %slice-start.3 = ((s8[13107200]{0:T(1024)(128)(4,1)}), s8[524288]{0:T(1024)(128)(4,1)S(1)}, s32[]{:S(2)}) async-start(s8[13107200]{0:T(1024)(128)(4,1)} %bitcast.9), calls=%async_computation.3 | async-start | bytes 1048576

commit v2 on v1

--- a/solution.py
+++ b/solution.py
@@ -12,6 +12,7 @@
 S1, S2A, S2B, T1, T2A, T2B, A1, A1F, A2, A2F = range(10)
 KINDS = 10
 STAGES = 9
+SLOTS, SLOTS_F = 8, 4
 
 
 def halves(shape):
@@ -30,19 +31,21 @@
     return n, lambda i: (pl.ds(pl.multiple_of(i * (rows // n), 8), rows // n), slice(None))
 
 
-def kernel(side, layers, shapes, *refs):
+def kernel(side, layers, shapes, late, *refs):
     n = len(shapes)
-    gs, ws, ms, vs, outs, gouts = (refs[i * n : (i + 1) * n] for i in range(6))
-    scratch = refs[6 * n : -4]
+    gs, ws, ms, vs, outs, mouts, vouts = (refs[i * n : (i + 1) * n] for i in range(7))
+    passed = refs[7 * n : 7 * n + 4]
+    scratch = refs[7 * n + 4 : -4]
     send, recv, local, stored = refs[-4:]
     kinds = list(dict.fromkeys(shapes))
     per = len(scratch) // len(kinds)
     held = {shape: scratch[i * per : (i + 1) * per] for i, shape in enumerate(kinds)}
     jobs, seen = [], {shape: 0 for shape in kinds}
-    for which, shape in enumerate(shapes):
+    for which in sorted(range(n), key=lambda i: i in late):
         for layer in range(layers):
-            jobs.append((which, layer, shape, seen[shape]))
-            seen[shape] += 1
+            jobs.append((which, layer, shapes[which], seen[shapes[which]]))
+            seen[shapes[which]] += 1
+    first_late = len(jobs) - layers * len(late)
 
     me = lax.axis_index("dp")
     xy = (lax.div(me, side), lax.rem(me, side))
@@ -103,6 +106,10 @@
             src, dst, to = wn.at[slot, c], block(p, s), across
         elif kind == A1F:
             src, dst, to = block(p, at(s, -by), d, 1), block(p, at(s, -by), d, 1), across
+        elif kind == A2 and q >= first_late:
+            src, dst, to = row(p, 1 - d, 1), row(p, 1 - d, 1), along
+        elif q >= first_late:
+            src, dst, to = row(p, d, 1), passed[2 * c + d].at[q - first_late], along
         elif kind == A2:
             src, dst, to = row(p), row(p), along
         else:
@@ -154,10 +161,12 @@
         mine = outs[which].at[(layer, xy[0], xy[1], *halves(shape)[1](2 * c, 2))]
         return pltpu.make_async_copy(held[shape][9].at[slot, c], mine, stored.at[q, c, 2])
 
-    def gradient(q, c, h):
-        which, layer, shape, slot = jobs[q]
-        mine = gouts[which].at[(layer, *halves(shape)[1](2 * c + h))]
-        return pltpu.make_async_copy(held[shape][3].at[slot, c, 0, h], mine, stored.at[q, c, h])
+    def moments(q):
+        which, layer, shape, slot = jobs[q]
+        return [
+            pltpu.make_async_copy(buffer.at[slot % 2], out[which].at[layer], stored.at[q, i, 0])
+            for i, (buffer, out) in enumerate(zip(held[shape][6:8], (mouts, vouts), strict=True))
+        ]
 
     def walk(shape, body):
         steps, piece = pieces(halves(shape)[0])
@@ -208,6 +217,9 @@
             start(q, T1)
             start(q, T2A)
         elif k == 3:
+            if slot >= 2:
+                for one in moments(next(i for i, job in enumerate(jobs) if job[2:] == (shape, slot - 2))):
+                    one.wait()
             for one in state(q):
                 one.start()
             for c, d in each:
@@ -238,13 +250,13 @@
                             return tuple(full)
 
                         g = functools.reduce(lambda a, b: a + b, [t[(*lead, *where)].astype(jnp.float32) for t, lead in terms])
-                        g16 = g.astype(jnp.bfloat16)
-                        g = g16.astype(jnp.float32)
-                        q2[(slot, c, 0, h, *where)] = g16
+                        g = g.astype(jnp.bfloat16).astype(jnp.float32)
                         there = (slot % 2, *shifted(offsets))
                         w = wb[there].astype(jnp.float32)
                         m = 0.9 * mb[there] + 0.1 * g
                         v = 0.95 * vb[there] + 0.05 * g * g
+                        mb[there] = m
+                        vb[there] = v
                         new = w - 0.02 * (m * lax.rsqrt(v + 1e-8) + 0.1 * w)
                         wn[(slot, c, *shifted(half))] = new.astype(jnp.bfloat16)
 
@@ -252,8 +264,8 @@
                 for d in range(2):
                     copy(q, c, d, A1).start()
                 weight(q, c).start()
-                for h in range(2):
-                    gradient(q, c, h).start()
+            for one in moments(q):
+                one.start()
         elif k == 5:
             arrived(q, A1)
             start(q, A1F)
@@ -261,10 +273,13 @@
             for c in range(2):
                 weight(q, c).wait()
             arrived(q, A1F)
+            if q >= first_late:
+                start(q, A2F)
             start(q, A2)
         elif k == 7:
             arrived(q, A2)
-            start(q, A2F)
+            if q < first_late:
+                start(q, A2F)
         else:
             arrived(q, A2F)
 
@@ -273,16 +288,16 @@
             if 0 <= t - k < len(jobs):
                 stage(k, t - k)
 
-    for q in range(len(jobs)):
-        for c in range(2):
-            for h in range(2):
-                gradient(q, c, h).wait()
+    for q, (_, _, shape, slot) in enumerate(jobs):
+        if slot + 2 >= seen[shape]:
+            for one in moments(q):
+                one.wait()
         for kind in range(KINDS):
             for c, d in each:
                 copy(q, c, d, kind).wait_send()
 
 
-def step_kernel(side, layers, shapes, terms, weights, m, v):
+def step_kernel(side, layers, shapes, late, terms, weights, m, v):
     scratch = []
     for shape in dict.fromkeys(shapes):
         count = layers * shapes.count(shape)
@@ -301,13 +316,15 @@
             pltpu.VMEM((count, 2, *both), jnp.bfloat16),
         ]
     jobs = layers * len(shapes)
+    passed = (layers * len(late), side, *halves(shapes[late[0]])[0])
     anywhere = pl.BlockSpec(memory_space=pl.ANY)
-    return pl.pallas_call(
-        functools.partial(kernel, side, layers, shapes),
+    outs = pl.pallas_call(
+        functools.partial(kernel, side, layers, shapes, late),
         out_shape=[jax.ShapeDtypeStruct(w.shape, jnp.bfloat16) for w in weights]
-        + [jax.ShapeDtypeStruct(one.shape, jnp.bfloat16) for one in m],
+        + [jax.ShapeDtypeStruct(one.shape, jnp.float32) for one in (*m, *v)]
+        + [jax.ShapeDtypeStruct(passed, jnp.bfloat16)] * 4,
         in_specs=[anywhere] * (4 * len(shapes)),
-        out_specs=[anywhere] * (2 * len(shapes)),
+        out_specs=[anywhere] * (3 * len(shapes) + 4),
         scratch_shapes=scratch
         + [
             pltpu.SemaphoreType.DMA((jobs, 2, 2, KINDS)),
@@ -318,6 +335,84 @@
         compiler_params=pltpu.CompilerParams(collective_id=0, has_side_effects=True, vmem_limit_bytes=67_043_328),
         name="step",
     )(*terms, *weights, *m, *v)
+    return outs[:-4], outs[-4:]
+
+
+def move(moves, slots, sems):
+    inward, outward = sems
+    used = {}
+    plan = []
+    for i, (src, dst, name) in enumerate(moves):
+        buffer = slots[name]
+        turn = used.setdefault(name, [])
+        place = buffer.at[len(turn) % buffer.shape[0]]
+        before = turn[-buffer.shape[0]] if len(turn) >= buffer.shape[0] else None
+        turn.append(i)
+        plan.append((functools.partial(pltpu.make_async_copy, src, place, inward.at[i]), functools.partial(pltpu.make_async_copy, place, dst, outward.at[i]), before))
+    done = set()
+    ahead = 0
+    for i in range(len(plan)):
+        while ahead < len(plan) and (plan[ahead][2] is None or plan[ahead][2] < i - 2 or ahead == i):
+            fetch, _, before = plan[ahead]
+            if before is not None:
+                plan[before][1]().wait()
+                done.add(before)
+            fetch().start()
+            ahead += 1
+        plan[i][0]().wait()
+        plan[i][1]().start()
+    for i in range(len(plan)):
+        if i not in done:
+            plan[i][1]().wait()
+
+
+def chunks(side, layers, shapes, late, wanted):
+    for which, shape in sorted(enumerate(shapes), key=lambda one: one[0] in late):
+        for layer in range(layers):
+            turn = late.index(which) * layers + layer if which in late else None
+            for c in range(2):
+                for h in range(2):
+                    for by in range(side):
+                        arrives = (by == 2) and turn is not None
+                        if arrives == wanted:
+                            yield which, layer, turn, c, h, by
+
+
+def settle(side, layers, shapes, late, *refs):
+    n = len(shapes)
+    temps, news = refs[: 3 * n], refs[3 * n + 4 : 6 * n + 4]
+    passed = refs[3 * n : 3 * n + 4]
+    *slots, inward, outward = refs[6 * n + 4 :]
+    kinds = list(dict.fromkeys(shapes))
+    me = lax.axis_index("dp")
+    xy = (lax.div(me, side), lax.rem(me, side))
+    moves = []
+    for i in range(n, 3 * n):
+        for layer in range(layers):
+            moves.append((temps[i].at[layer], news[i].at[layer], ("f", shapes[i % n])))
+    for which, layer, turn, c, h, by in chunks(side, layers, shapes, late, False):
+        quarter = halves(shapes[which])[1](2 * c + h)
+        i = lax.rem(xy[c] + by, side)
+        there = (layer, i, slice(None), *quarter) if c == 0 else (layer, slice(None), i, *quarter)
+        behind = side - 1 if h == 0 else 1
+        src = passed[2 * c + h].at[turn] if turn is not None and by == behind else temps[which].at[there]
+        moves.append((src, news[which].at[there], ("b", shapes[which])))
+    move(moves, dict(zip([(a, k) for k in kinds for a in "bf"], slots, strict=True)), (inward, outward))
+
+
+def place(side, layers, shapes, late, *refs):
+    n = len(late)
+    came, news = refs[n : n + 4], refs[n + 4 : 2 * n + 4]
+    slots, inward, outward = refs[2 * n + 4 :]
+    me = lax.axis_index("dp")
+    xy = (lax.div(me, side), lax.rem(me, side))
+    moves = []
+    for which, layer, turn, c, h, by in chunks(side, layers, shapes, late, True):
+        quarter = halves(shapes[which])[1](2 * c + h)
+        i = lax.rem(xy[c] + by, side)
+        there = (layer, i, slice(None), *quarter) if c == 0 else (layer, slice(None), i, *quarter)
+        moves.append((came[2 * c + h].at[turn], news[late.index(which)].at[there], "b"))
+    move(moves, {"b": slots}, (inward, outward))
 
 
 def solution(mesh):
@@ -327,23 +422,62 @@
         terms, weights, m, v = (arrays[i : i + 3] for i in (0, 3, 6, 9))
         shapes = tuple(one.shape[1:] for one in m)
         layers = m[0].shape[0]
+        late = tuple(i for i, shape in enumerate(shapes) if shape == shapes[0])
         split = [(layers, side, side, *shape) for shape in shapes]
-        *new, g0, g1, g2 = step_kernel(
+        temps, passed = step_kernel(
             side,
             layers,
             shapes,
+            late,
             [t[0].reshape(s) for t, s in zip(terms, split, strict=True)],
             [w.reshape(s) for w, s in zip(weights, split, strict=True)],
             m,
             v,
         )
-        whole = [one.reshape(w.shape) for one, w in zip(new, weights, strict=True)]
-        g = [one.astype(jnp.float32) for one in (g0, g1, g2)]
-        return (
-            *whole,
-            *(0.9 * a + 0.1 * b for a, b in zip(m, g, strict=True)),
-            *(0.95 * a + 0.05 * b * b for a, b in zip(v, g, strict=True)),
-        )
+        came = []
+        for c in range(2):
+            for by in (1, -1):
+                ring = []
+                for i in range(side):
+                    for j in range(side):
+                        to = ((i + by) % side, j) if c == 0 else (i, (j + by) % side)
+                        ring.append((i * side + j, to[0] * side + to[1]))
+                came.append(lax.ppermute(passed[len(came)], "dp", ring))
+        anywhere = pl.BlockSpec(memory_space=pl.ANY)
+        kinds = list(dict.fromkeys(shapes))
+        slots = []
+        for shape in kinds:
+            slots += [pltpu.VMEM((SLOTS, side, *halves(shape)[0]), jnp.bfloat16), pltpu.VMEM((SLOTS_F, *shape), jnp.float32)]
+        count = len(list(chunks(side, layers, shapes, late, False))) + 2 * len(shapes) * layers
+        bytes_moved = 2 * sum(one.size * one.dtype.itemsize for one in temps)
+        new = list(pl.pallas_call(
+            functools.partial(settle, side, layers, shapes, late),
+            out_shape=[jax.ShapeDtypeStruct(one.shape, one.dtype) for one in temps],
+            in_specs=[anywhere] * (len(temps) + 4),
+            out_specs=[anywhere] * len(temps),
+            scratch_shapes=[*slots, pltpu.SemaphoreType.DMA((count,)), pltpu.SemaphoreType.DMA((count,))],
+            compiler_params=pltpu.CompilerParams(vmem_limit_bytes=67_043_328),
+            cost_estimate=pl.CostEstimate(flops=10**9, bytes_accessed=bytes_moved, transcendentals=0),
+            name="settle",
+        )(*temps, *passed))
+        arriving = len(list(chunks(side, layers, shapes, late, True)))
+        last = pl.pallas_call(
+            functools.partial(place, side, layers, shapes, late),
+            out_shape=[jax.ShapeDtypeStruct(new[i].shape, new[i].dtype) for i in late],
+            in_specs=[anywhere] * (len(late) + 4),
+            out_specs=[anywhere] * len(late),
+            scratch_shapes=[
+                pltpu.VMEM((arriving, side, *halves(shapes[0])[0]), jnp.bfloat16),
+                pltpu.SemaphoreType.DMA((arriving,)),
+                pltpu.SemaphoreType.DMA((arriving,)),
+            ],
+            input_output_aliases={i: i for i in range(len(late))},
+            compiler_params=pltpu.CompilerParams(vmem_limit_bytes=67_043_328),
+            name="place",
+        )(*[new[i] for i in late], *came)
+        for i, one in zip(late, last, strict=True):
+            new[i] = one
+        return (*(one.reshape(w.shape) for one, w in zip(new[:3], weights, strict=True)), *new[3:])
 
     all_of, cut = P(None, None, None), P(None, "dp", None)
     return jax.shard_map(

time: 445 us -> 421 us (0.946)
  local copies, waits for them, and re-layouts: 23 us -> 0 us
  other arithmetic: 12 us -> 0 us
  starting transfers between devices: 0 us -> 5.43 us
    unnamed x17 -> x0, local copies, waits for them, and re-layouts: 23 us -> none
    add x2 -> x0, other arithmetic: 12 us -> none  [step(): 0.95 * a + 0.05 * b * b]
    ppermute x0 -> x4, starting transfers between devices: none -> 5.43 us  [step(): came.append(lax.ppermute(passed[len(came)], 'dp', ring))]
    pallas_call x1 -> x3, Pallas kernels: 409 us -> 410 us  [the longest x1 374 us: step_kernel(): pl.pallas_call(functools.partial(kernel, side, layers, shapes, late), out...]
  transfers between devices with their start and end apart: 0 -> 4, of which waited for: 0 -> 2; matrix products, arithmetic and copies ran while one was open for 0% -> 0% of each run, Pallas kernels for 0% -> 7%
where the time goes in v2:
time: 421 us; the launch traced here: 420 us
  Pallas kernels  410 us (97%)
  starting transfers between devices  5.43 us (1%)
    pallas_call x1, Pallas kernels, step_kernel(): pl.pallas_call(functools.partial(kernel, side, layers, shapes, late), out...  374 us
    pallas_call x1, Pallas kernels, step(): pl.pallas_call(functools.partial(settle, side, layers, shapes, late), out...  30.4 us
  transfers between devices with their start and end apart: 4, of which 2 were waited for; matrix products, arithmetic and copies ran while one was open for 0% of the time, Pallas kernels for 7%

profile of v2, /device:TPU:97, one launch (start us, length us, event | category | flops | bytes accessed | tf_op | source)
XLA Modules:
  0.0 419.8 jit_solution(15753636703460472142)
XLA Ops:
  0.6 374.0 %step.1 = (bf16[2,4,4,64,3200]{4,3,2,1,0:T(8,128)(2,1)}, bf16[2,4,4,64,3200]{4,3,2,1,0:T(8,128)(2,1)}, bf16[2,4,4,200,1024]{4,3,2,1,0:T(8,128)(2,1)}, f32[2,64,3...) custom-call(bf16[2,4,4,64,3200]{4,3,2,1,0:T(8,128)(2,1)} %bitcast.11, ...), custom_call_target="tpu_custom_call" | custom-call | tf_op jit(solution)/shard_map/step/pallas_call | solution.py:321
  374.6 0.1 collective-permute-start
  374.7 2.6 collective-permute-start.1
  377.4 0.0 collective-permute-start.2
  377.4 2.7 collective-permute-start.3
  380.1 30.4 %settle.1 = (bf16[2,4,4,64,3200]{4,3,2,1,0:T(8,128)(2,1)}, bf16[2,4,4,64,3200]{4,3,2,1,0:T(8,128)(2,1)}, bf16[2,4,4,200,1024]{4,3,2,1,0:T(8,128)(2,1)}, f32[2,64...) custom-call(bf16[2,4,4,64,3200]{4,3,2,1,0:T(8,128)(2,1)} %get-tuple-, ...), custom_call_target="tpu_custom_call" | custom-call | flops 1000000000 | bytes 98304000 | tf_op jit(solution)/shard_map/settle/pallas_call | solution.py:453
  410.5 1.5 collective-permute-done.refs_2_
  412.0 0.0 collective-permute-done.1.refs_3_
  412.0 2.1 collective-permute-done.2.refs_4_
  414.1 0.0 collective-permute-done.3.refs_5_
  414.1 5.6 %place.1 = (bf16[2,4,4,64,3200]{4,3,2,1,0:T(8,128)(2,1)}, bf16[2,4,4,64,3200]{4,3,2,1,0:T(8,128)(2,1)}) custom-call(bf16[2,4,4,64,3200]{4,3,2,1,0:T(8,128)(2,1)} %get-tuple-element.46.refs_0_, bf16[2,4,4,64,3200]{4,3,2,1,0:T(8,128)(2,1)} %get-tuple-element.47.refs_1_, ...), custom_call_target="tpu_custom_call", output_to_operand_aliasing={{0}: (0, {}), {1}: (1, {})} | custom-call | tf_op jit(solution)/shard_map/place/pallas_call | solution.py:464
Async XLA Ops:
  374.6 37.4 %collective-permute-start = (bf16[4,4,16,3200]{3,2,1,0:T(8,128)(2,1)}, bf16[4,4,16,3200]{3,2,1,0:T(8,128)(2,1)}, u32[]{:S(2)}, u32[]{:S(2)}) collective-permute-start(bf16[4,4,16,3200]{3,2,1,0:T(8,128)(2,1)} %get-tuple-element.42.refs_9_), channel_id=1, source_target_pairs={{0,4},{1,5},{2,6},{3,7},{4,8},{5,9},{6,10},{7,11},{8,12},{9,13},{1... | collective-permute-start | bytes 4915208 | tf_op jit(solution)/shard_map/ppermute | solution.py:445
  374.7 37.3 %collective-permute-start.1 = (bf16[4,4,16,3200]{3,2,1,0:T(8,128)(2,1)}, bf16[4,4,16,3200]{3,2,1,0:T(8,128)(2,1)}, u32[]{:S(2)}, u32[]{:S(2)}) collective-permute-start(bf16[4,4,16,3200]{3,2,1,0:T(8,128)(2,1)} %get-tuple-element.43.refs_10_), channel_id=1, source_target_pairs={{0,12},{1,13},{2,14},{3,15},{4,0},{5,1},{6,2},{7,3},{8,4},{9,5},{1... | collective-permute-start | bytes 4915208 | tf_op jit(solution)/shard_map/ppermute | solution.py:445
  377.4 36.8 %collective-permute-start.2 = (bf16[4,4,16,3200]{3,2,1,0:T(8,128)(2,1)}, bf16[4,4,16,3200]{3,2,1,0:T(8,128)(2,1)}, u32[]{:S(2)}, u32[]{:S(2)}) collective-permute-start(bf16[4,4,16,3200]{3,2,1,0:T(8,128)(2,1)} %get-tuple-element.44.refs_11_), channel_id=1, source_target_pairs={{0,1},{1,2},{2,3},{3,0},{4,5},{5,6},{6,7},{7,4},{8,9},{9,10},{10,1... | collective-permute-start | bytes 4915208 | tf_op jit(solution)/shard_map/ppermute | solution.py:445
  377.4 36.8 %collective-permute-start.3 = (bf16[4,4,16,3200]{3,2,1,0:T(8,128)(2,1)}, bf16[4,4,16,3200]{3,2,1,0:T(8,128)(2,1)}, u32[]{:S(2)}, u32[]{:S(2)}) collective-permute-start(bf16[4,4,16,3200]{3,2,1,0:T(8,128)(2,1)} %get-tuple-element.45.refs_12_), channel_id=1, source_target_pairs={{0,3},{1,0},{2,1},{3,2},{4,7},{5,4},{6,5},{7,6},{8,11},{9,8},{10,9... | collective-permute-start | bytes 4915208 | tf_op jit(solution)/shard_map/ppermute | solution.py:445
